TPU v7x, 256 devices: a whole 4x4x8 slice. The times are simulated.
256 devices in a mesh: row: 32 (over y, z), col: 8 (over x, core).
Axes of the slice: x: 4, y: 4, z: 8, core: 2. Of those that a mesh axis runs over, the one named last changes fastest.
Arguments:
- features: bfloat16 [49152, 4096], P(('row', 'col')), may hold values from -24 to 24
- cotangent: bfloat16 [49152, 8192], P(('row', 'col')), may hold values from -0.02734375 to 0.02734375
Outputs:
- weight_grad: float32 [4096, 8192], P('row', 'col')
All inputs are finite; a program needn't handle non-finite values.
Results may differ from a plain program's by a relative error of at most 0.0003.
Values may be sent and summed in bfloat16 or wider, within the bound.
A program may use at most 256 MiB of HBM per device.

v0:
```python
import jax
import jax.numpy as jnp
from jax import lax
from jax.sharding import Mesh
from jax.sharding import PartitionSpec as P

ROW = ("row_0", "row_1")
ROW_COL = ("row_0", "row_1", "col")


def sum_by_axis(array, axes, dim):
    for axis in axes:
        array = lax.psum_scatter(array, axis, scatter_dimension=dim, tiled=True)
    return array


def tokens_product(left, right):
    return lax.dot_general(
        left, right, (((0,), (0,)), ((), ())), preferred_element_type=jnp.float32
    )


def local(features, cotangent):
    columns = lax.all_to_all(cotangent, "col", split_axis=1, concat_axis=0, tiled=True)
    partial_value = tokens_product(lax.all_gather(features, "col", axis=0, tiled=True), columns)
    return sum_by_axis(partial_value, ROW, 0)


def solution(mesh):
    torus = Mesh(mesh.devices.reshape(4, 8, mesh.shape["col"]), ("row_0", "row_1", "col"))
    in_specs = (P(ROW_COL, None), P(ROW_COL, None))
    out_specs = P(ROW, "col")
    return jax.shard_map(local, mesh=torus, in_specs=in_specs, out_specs=out_specs, check_vma=False)
```

profile of v0, /device:TPU:1, one launch (start us, length us, event | category | flops | bytes accessed | tf_op | source)
XLA Modules:
  0.0 340.8 jit_solution(15472205882023542649)
XLA Ops:
  6.5 0.0 all-gather.2.cloned.1.call-start
  6.5 0.7 all-gather.2.cloned.1.call-update
  7.3 0.0 reduce-scatter.3.cloned.1.call-start
  7.3 2.3 copy.7
  9.6 65.5 %all_to_all.19 = bf16[192,8,1024]{2,0,1:T(8,128)(2,1)S(1)} all-to-all(bf16[192,8,1024]{2,0,1:T(8,128)(2,1)S(1)} %bitcast.9), channel_id=1, replica_groups=mesh['row_0'=4,'row_1'=8,'col'=8] {'col'}, dimensions={1} | all-to-all | bytes 6291456 | tf_op jit(solution)/shard_map/all_to_all | solution.py:24
  75.1 30.6 %all-gather.2.cloned.1.call-done = bf16[1536,4096]{1,0:T(8,128)(2,1)} async-done(((bf16[192,4096]{1,0:T(8,128)(2,1)}), bf16[1536,4096]{1,0:T(8,128)(2,1)}) %all-gather.2.cloned.1.call-update) | async-done | bytes 12582928 | tf_op jit(solution)/shard_map/all_gather | solution.py:25
  105.7 19.5 %fusion = f32[4096,1024]{1,0:T(8,128)} fusion(bf16[1536,4096]{1,0:T(8,128)(2,1)} %all-gather.2.cloned.1.call-done, bf16[1536,1024]{1,0:T(8,128)(2,1)S(1)} %bitcast.11), kind=kOutput, calls=%fused_computation.1 | convolution fusion | flops 12884901888 | bytes 32505856 | tf_op jit(solution)/shard_map/dot_general | solution.py:18
  125.2 0.0 reduce-scatter.3.cloned.1.call-update
  125.3 0.0 reduce-scatter.5.cloned.1.call-start
  125.3 151.3 %reduce-scatter.3.cloned.1.call-done = f32[1024,1024]{1,0:T(8,128)} async-done(((f32[4096,1024]{1,0:T(8,128)}), f32[1024,1024]{1,0:T(8,128)}) %reduce-scatter.3.cloned.1.call-update) | async-done | bytes 4194320 | tf_op jit(solution)/shard_map/reduce_scatter | solution.py:13
  276.6 0.0 reduce-scatter.5.cloned.1.call-update
  276.6 57.6 %reduce-scatter.5.cloned.1.call-done = f32[128,1024]{1,0:T(8,128)} async-done(((f32[1024,1024]{1,0:T(8,128)}), f32[128,1024]{1,0:T(8,128)}) %reduce-scatter.5.cloned.1.call-update) | async-done | bytes 524304 | tf_op jit(solution)/shard_map/reduce_scatter | solution.py:13
Async XLA Ops:
  6.5 99.2 %all-gather.2.cloned.1.call-start = ((), (), s32[]{:S(2)}) async-start(), calls=%async_computation.3 | async-start | bytes 14155776 | tf_op jit(solution)/shard_map/all_gather | solution.py:25
  7.3 269.4 %reduce-scatter.3.cloned.1.call-start = ((), (), s32[]{:S(2)}) async-start(), calls=%async_computation.4 | async-start | bytes 20971520 | tf_op jit(solution)/shard_map/reduce_scatter | solution.py:13
  125.3 209.0 %reduce-scatter.5.cloned.1.call-start = ((), (), s32[]{:S(2)}) async-start(), calls=%async_computation.5 | async-start | bytes 4718592 | tf_op jit(solution)/shard_map/reduce_scatter | solution.py:13
Sparse Core Ops, SparseCore 0:
  9.2 96.4 all-gather.1
  125.4 151.1 reduce-scatter.2
  279.2 55.0 reduce-scatter.4
where the time goes:
time: 341 us
  waiting for transfers between devices  240 us (70%)
  blocking collectives  65.5 us (19%)
  matrix products  19.5 us (6%)
  between operations  13.1 us (4%)
    reduce_scatter x2, waiting for transfers between devices, sum_by_axis(): array = lax.psum_scatter(array, axis, scatter_dimension=dim, tiled=True)  209 us
    all_to_all x1, blocking collectives, local(): lax.all_to_all(cotangent, 'col', split_axis=1, concat_axis=0, tiled=True)  65.5 us
    all_gather x1, waiting for transfers between devices, local(): lax.all_gather(features, 'col', axis=0, tiled=True)  30.6 us
    dot_general x1, matrix products, tokens_product(): lax.dot_general(left, right, (((0,), (0,)), ((), ())), preferred_element_...  19.5 us
  transfers between devices with their start and end apart: 3, of which 3 were waited for; matrix products, arithmetic and copies ran while one was open for 1% of the time, Pallas kernels for 0%

commit v1 on v0

--- a/solution.py
+++ b/solution.py
@@ -22,7 +22,20 @@
 
 def local(features, cotangent):
     columns = lax.all_to_all(cotangent, "col", split_axis=1, concat_axis=0, tiled=True)
-    partial_value = tokens_product(lax.all_gather(features, "col", axis=0, tiled=True), columns)
+
+    def run_classes(own_rows, a_name):
+        carry = jnp.concatenate(
+            lax.all_to_all(
+                jnp.stack([own_rows] * lax.psum(1, axis_name=a_name), axis=0),
+                split_axis=0,
+                axis_name=a_name,
+                concat_axis=0,
+            ),
+            0,
+        )
+        return carry
+
+    partial_value = tokens_product(run_classes(features, a_name="col"), columns)
     return sum_by_axis(partial_value, ROW, 0)
 
 

time: 341 us -> 437 us (1.28)
  blocking collectives: 65.5 us -> 187 us
  waiting for transfers between devices: 240 us -> 211 us
  local copies, waits for them, and re-layouts: 2.32 us -> 9.88 us
    all_to_all x0 -> x1, blocking collectives: none -> 144 us  [run_classes(): lax.all_to_all(jnp.stack([own_rows] * lax.psum(1, axis_name=a_name), axis...]
    all_gather x1 -> x0, waiting for transfers between devices: 30.6 us -> none  [local(): lax.all_gather(features, 'col', axis=0, tiled=True)]
    all_to_all x1, blocking collectives: 65.5 us -> 43.1 us  [local(): lax.all_to_all(cotangent, 'col', split_axis=1, concat_axis=0, tiled=True)]
    another operation x0 -> x1, local copies, waits for them, and re-layouts: none -> 7.56 us  [run_classes(): jnp.stack([own_rows] * lax.psum(1, axis_name=a_name), axis=0)]
  transfers between devices with their start and end apart: 3 -> 2, of which waited for: 3 -> 2; matrix products, arithmetic and copies ran while one was open for 1% -> 0% of each run, Pallas kernels for 0% -> 0%
where the time goes in v1:
time: 437 us
  waiting for transfers between devices  211 us (48%)
  blocking collectives  187 us (43%)
  matrix products  16.2 us (4%)
  between operations  13.4 us (3%)
  local copies, waits for them, and re-layouts  9.88 us (2%)
    reduce_scatter x2, waiting for transfers between devices, sum_by_axis(): array = lax.psum_scatter(array, axis, scatter_dimension=dim, tiled=True)  211 us
    all_to_all x1, blocking collectives, run_classes(): lax.all_to_all(jnp.stack([own_rows] * lax.psum(1, axis_name=a_name), axis...  144 us
    all_to_all x1, blocking collectives, local(): lax.all_to_all(cotangent, 'col', split_axis=1, concat_axis=0, tiled=True)  43.1 us
    dot_general x1, matrix products, tokens_product(): lax.dot_general(left, right, (((0,), (0,)), ((), ())), preferred_element_...  16.2 us
  transfers between devices with their start and end apart: 2, of which 2 were waited for; matrix products, arithmetic and copies ran while one was open for 0% of the time, Pallas kernels for 0%

profile of v1, /device:TPU:1, one launch (start us, length us, event | category | flops | bytes accessed | tf_op | source)
XLA Modules:
  0.0 436.9 jit_solution(16523650074647787561)
XLA Ops:
  6.5 0.0 reduce-scatter.3.cloned.1.call-start
  6.5 2.3 copy.6
  8.9 43.1 %all_to_all.21 = bf16[192,8,1024]{2,0,1:T(8,128)(2,1)S(1)} all-to-all(bf16[192,8,1024]{2,0,1:T(8,128)(2,1)S(1)} %bitcast.10), channel_id=1, replica_groups=mesh['row_0'=4,'row_1'=8,'col'=8] {'col'}, dimensions={1} | all-to-all | bytes 6291456 | tf_op jit(solution)/shard_map/all_to_all | solution.py:24
  51.9 7.6 %stack.2 = bf16[8,192,4096]{2,1,0:T(8,128)(2,1)} broadcast(bf16[192,4096]{1,0:T(8,128)(2,1)} %param.2), dimensions={1,2} | broadcast | bytes 14155776 | tf_op jit(solution)/shard_map/stack | solution.py:29
  59.5 143.5 %all_to_all.22 = bf16[8,192,4096]{2,1,0:T(8,128)(2,1)S(1)} all-to-all(bf16[8,192,4096]{2,1,0:T(8,128)(2,1)} %stack.2), channel_id=1, replica_groups=mesh['row_0'=4,'row_1'=8,'col'=8] {'col'}, dimensions={0} | all-to-all | bytes 25165824 | tf_op jit(solution)/shard_map/all_to_all | solution.py:28
  203.0 16.2 %convolution_bitcast_fusion = f32[4096,1024]{1,0:T(8,128)} fusion(bf16[8,192,4096]{2,1,0:T(8,128)(2,1)S(1)} %all_to_all.22, bf16[192,8,1024]{2,0,1:T(8,128)(2,1)S(1)} %all_to_all.21), kind=kOutput, calls=%fused_computation | convolution fusion | flops 12884901888 | bytes 32505856 | tf_op jit(solution)/shard_map/dot_general | solution.py:18
  219.2 0.0 reduce-scatter.3.cloned.1.call-update
  219.2 0.0 reduce-scatter.5.cloned.1.call-start
  219.3 153.2 %reduce-scatter.3.cloned.1.call-done = f32[1024,1024]{1,0:T(8,128)} async-done(((f32[4096,1024]{1,0:T(8,128)}), f32[1024,1024]{1,0:T(8,128)}) %reduce-scatter.3.cloned.1.call-update) | async-done | bytes 4194320 | tf_op jit(solution)/shard_map/reduce_scatter | solution.py:13
  372.5 0.0 reduce-scatter.5.cloned.1.call-update
  372.5 57.6 %reduce-scatter.5.cloned.1.call-done = f32[128,1024]{1,0:T(8,128)} async-done(((f32[1024,1024]{1,0:T(8,128)}), f32[128,1024]{1,0:T(8,128)}) %reduce-scatter.5.cloned.1.call-update) | async-done | bytes 524304 | tf_op jit(solution)/shard_map/reduce_scatter | solution.py:13
Async XLA Ops:
  6.5 365.9 %reduce-scatter.3.cloned.1.call-start = ((), (), s32[]{:S(2)}) async-start(), calls=%async_computation.4 | async-start | bytes 20971520 | tf_op jit(solution)/shard_map/reduce_scatter | solution.py:13
  219.2 210.8 %reduce-scatter.5.cloned.1.call-start = ((), (), s32[]{:S(2)}) async-start(), calls=%async_computation.5 | async-start | bytes 4718592 | tf_op jit(solution)/shard_map/reduce_scatter | solution.py:13
Sparse Core Ops, SparseCore 0:
  219.4 153.0 reduce-scatter.2
  375.0 55.0 reduce-scatter.4
